TPU v7x, 32 devices: a whole 2x2x4 slice. The times are simulated.
32 devices in a mesh: samp: 8 (over y, x, core), cpg: 4 (over z).
Axes of the slice: x: 2, y: 2, z: 4, core: 2. Of those that a mesh axis runs over, the one named last changes fastest.
Arguments:
- responses: bfloat16 [256, 16384], P('samp', 'cpg'), may hold values from -5 to 5
- weights: bfloat16 [256, 16384], P('samp', 'cpg'), may hold values from 1 to 8
- phenotype: float32 [16384], P('cpg'), may hold values from -6 to 6
- eigvecs: bfloat16 [16384, 16384], P('cpg', 'samp'), may hold values from -0.046875 to 0.046875
- eigvals: float32 [16384], P('samp'), may hold values from 0.0001 to 1
- positions: int32 [256], replicated, may hold values from 1 to 76800, as said below
- reaches: int32 [256], P('cpg'), may hold values from 1 to 8
Outputs:
- smoothed: float32 [256], P('cpg')
- log_scale: float32 [256], P('cpg')
Inputs may be any that keep to these rules, and one draw needn't show every extreme that they name: CpG m (from 0) lies at 300 m plus an offset of 1 to 300, so positions strictly increase and consecutive CpGs lie 1 to 599 base pairs apart.
All inputs are finite; a program needn't handle non-finite values.
Results may differ from a plain program's by a relative error of at most 0.0041.
Values may be sent and summed in bfloat16 or wider, within the bound.
A program may use at most 64 MiB of HBM per device.

v0:
```python
import jax
import jax.numpy as jnp
from jax import lax
from jax.sharding import PartitionSpec as P

ITERS = 4
HALO = 8
EPSILON = 1e-06
band_width = 1000.0


def padded(value, sides, width):
    for axis, dim in sides:
        peers, length = (lax.axis_size(axis), value.shape[dim])
        up = [(i, (i + 1) % peers) for i in range(peers - 1)]
        down = [(j, i) for i, j in up]
        last = lax.slice_in_dim(value, length - width, length, axis=dim)
        leading = lax.slice_in_dim(value, 0, width, axis=dim)
        before = lax.ppermute(last, axis, up)
        after = lax.ppermute(leading, axis, down)
        value = jnp.concatenate([before, value, after], axis=dim)
    return value


def smooth_block(widened, places, present, reaches):
    block_len = reaches.shape[0]
    centre = places[HALO : HALO + block_len]
    total_sum = jnp.zeros((block_len,), jnp.float32)
    norm_sum = jnp.zeros((block_len,), jnp.float32)
    for offset in range(2 * HALO + 1):
        near_scores = widened[offset : offset + block_len]
        near_places = places[offset : offset + block_len]
        within = (abs(offset - HALO) <= reaches).astype(jnp.float32)
        kernel = (
            present[offset : offset + block_len]
            * within
            * jnp.exp(-jnp.abs(near_places - centre) / band_width)
        )
        total_sum = total_sum + kernel * near_scores
        norm_sum = norm_sum + kernel
    return total_sum / norm_sum


def fit_scores(rot_resp, rot_design, eigen_part, sum_axis, fit_total, score_total):
    log_scale = jnp.zeros((rot_resp.shape[1 - sum_axis],), jnp.float32)
    for repeat in range(ITERS):
        inverse = 1.0 / (jnp.expand_dims(jnp.exp(log_scale), sum_axis) * eigen_part + 1.0)
        design_over = rot_design * inverse
        crossed_part = jnp.sum(design_over * rot_resp, axis=sum_axis)
        energy_part = jnp.sum(design_over * rot_design, axis=sum_axis)
        leverage = eigen_part * inverse
        traced_part = jnp.sum(leverage + 0.0 * inverse, axis=sum_axis)
        fisher_part = jnp.sum(leverage * leverage, axis=sum_axis)
        scaled = leverage * inverse
        resp_part = jnp.sum(scaled * rot_resp * rot_resp, axis=sum_axis)
        mixed_part = jnp.sum(scaled * rot_design * rot_resp, axis=sum_axis)
        design_part = jnp.sum(scaled * rot_design * rot_design, axis=sum_axis)
        crossed, energy, traced, fisher, resp_spread, mixed_spread, design_spread = fit_total(
            (
                crossed_part,
                energy_part,
                traced_part,
                fisher_part,
                resp_part,
                mixed_part,
                design_part,
            )
        )
        energy = energy + EPSILON
        effect = crossed / energy
        spread = resp_spread - 2.0 * effect * mixed_spread + effect * effect * design_spread
        gradient = 0.5 * (spread - traced)
        log_scale = log_scale + jnp.tanh(gradient / (jnp.exp(log_scale) * (0.5 * fisher)))
    inverse = 1.0 / (jnp.expand_dims(jnp.exp(log_scale), sum_axis) * eigen_part + 1.0)
    design_over = rot_design * inverse
    crossed, energy = score_total(
        (
            jnp.sum(design_over * rot_resp, axis=sum_axis),
            jnp.sum(design_over * rot_design, axis=sum_axis),
        )
    )
    return (crossed / jnp.sqrt(energy + EPSILON), log_scale)


def shards(responses, weights, phenotype, eigvecs, eigvals, positions, reaches):
    root_weight = jnp.sqrt(weights.astype(jnp.float32))
    weighted = (root_weight * responses.astype(jnp.float32)).astype(jnp.bfloat16)
    design = (root_weight * phenotype[None, :]).astype(jnp.bfloat16)
    all_resp, all_design = (
        lax.all_gather(weighted, "samp", axis=0, tiled=True),
        lax.all_gather(design, "samp", axis=0, tiled=True),
    )
    cpg_count = lax.axis_size("cpg")
    block_len = reaches.shape[0]
    total_cpgs = block_len * cpg_count
    base = lax.axis_index("cpg") * block_len

    def fit_block(partials):
        return lax.psum(partials, "samp")

    def score_block(partials):
        return lax.psum(partials, "samp")

    rotated = lax.psum_scatter(
        jnp.concatenate(
            [
                jnp.dot(all_resp, eigvecs, preferred_element_type=jnp.float32),
                jnp.dot(all_design, eigvecs, preferred_element_type=jnp.float32),
            ],
            axis=1,
        ),
        "cpg",
        scatter_dimension=0,
        tiled=True,
    )
    comp_width = eigvecs.shape[1]
    scores, log_scale = fit_scores(
        rotated[:, :comp_width],
        rotated[:, comp_width:],
        eigvals[None, :],
        1,
        fit_block,
        score_block,
    )
    widened = padded(scores, (("cpg", 0),), HALO)
    places = lax.dynamic_slice_in_dim(
        jnp.pad(positions.astype(jnp.float32), HALO), base, block_len + 2 * HALO, 0
    )
    global_index = base - HALO + jnp.arange(block_len + 2 * HALO, dtype=jnp.int32)
    present = ((global_index >= 0) & (global_index < total_cpgs)).astype(jnp.float32)
    smoothed = smooth_block(widened, places, present, reaches)
    return (smoothed, log_scale)


def solution(mesh):
    in_specs = (
        P("samp", "cpg"),
        P("samp", "cpg"),
        P("cpg"),
        P("cpg", "samp"),
        P("samp"),
        P(),
        P("cpg"),
    )
    out_specs = (P("cpg"), P("cpg"))
    return jax.shard_map(shards, mesh=mesh, in_specs=in_specs, out_specs=out_specs, check_vma=False)
```

profile of v0, /device:TPU:0, one launch (start us, length us, event | category | flops | bytes accessed | tf_op | source)
XLA Modules:
  0.0 242.1 jit_solution(15517261634825529933)
XLA Ops:
  7.2 2.0 multiply_convert_fusion.1
  9.3 0.7 all-gather.5.cloned.1.call-update
  10.1 30.3 %all-gather.3.cloned.1.call-done = bf16[256,4096]{1,0:T(8,128)(2,1)} async-done(((bf16[32,4096]{1,0:T(8,128)(2,1)}), bf16[256,4096]{1,0:T(8,128)(2,1)}) %all-gather.3.cloned.1.call-update) | async-done | bytes 2097168 | tf_op jit(solution)/shard_map/all_gather | solution.py:90
  40.4 8.7 %fusion.38 = f32[256,2048]{1,0:T(8,128)S(1)} fusion(bf16[256,4096]{1,0:T(8,128)(2,1)} %all-gather.3.cloned.1.call-done, bf16[4096,2048]{1,0:T(8,128)(2,1)} %param.10), kind=kOutput, calls=%fused_computation.110 | convolution fusion | flops 4294967296 | bytes 20971520 | tf_op jit(solution)/shard_map/dot_general | solution.py:107
  49.1 21.0 %all-gather.5.cloned.1.call-done = bf16[256,4096]{1,0:T(8,128)(2,1)} async-done(((bf16[32,4096]{1,0:T(8,128)(2,1)}), bf16[256,4096]{1,0:T(8,128)(2,1)}) %all-gather.5.cloned.1.call-update) | async-done | bytes 2097168 | tf_op jit(solution)/shard_map/all_gather | solution.py:91
  70.1 8.7 %fusion.39 = f32[256,2048]{1,0:T(8,128)S(1)} fusion(bf16[256,4096]{1,0:T(8,128)(2,1)} %all-gather.5.cloned.1.call-done, bf16[4096,2048]{1,0:T(8,128)(2,1)} %param.10), kind=kOutput, calls=%fused_computation.111 | convolution fusion | flops 4294967296 | bytes 20971520 | tf_op jit(solution)/shard_map/dot_general | solution.py:108
  78.8 2.3 pad_maximum_fusion
  81.2 0.6 copy-done.2
  81.9 0.6 multiply_multiply_fusion.14
  82.5 75.6 %reduce-scatter.2.cloned.1.call-done = f32[64,4096]{1,0:T(8,128)} async-done(((f32[256,4096]{1,0:T(8,128)}), f32[64,4096]{1,0:T(8,128)}) %reduce-scatter.2.cloned.1.call-update) | async-done | bytes 1048592 | tf_op jit(solution)/shard_map/reduce_scatter | solution.py:104
  158.1 1.7 fusion.7
  159.8 0.7 reduce_sum.280
  160.5 0.6 reduce_sum.282
  161.1 13.3 %all-reduce.5 = (f32[64]{0:T(128)S(1)}, f32[64]{0:T(128)S(1)}, f32[64]{0:T(128)S(1)}, f32[64]{0:T(128)S(1)}, f32[64]{0:T(128)S(1)}, /*index=5*/f32[64]{0:T(128)S(1)}, f32[64]{0:T(128)S(1)}) all-reduce(f32[64]{0:T(128)S(1)} %reduce_sum.282, f32[64]{0:T(128)S(1)} %reduce_sum.280, ...), channel_id=1, replica_groups=mesh['samp'=8,'cpg'=4] {'samp'}, use_global_device_ids=true, to_apply=%region_14.0 | all-reduce | flops 448 | bytes 3584 | tf_op jit(solution)/shard_map/psum | solution.py:99
  174.4 1.9 multiply_reduce_fusion.12
  176.3 11.8 %all-reduce.4 = (f32[64]{0:T(128)S(1)}, f32[64]{0:T(128)S(1)}, f32[64]{0:T(128)S(1)}, f32[64]{0:T(128)S(1)}, f32[64]{0:T(128)S(1)}, /*index=5*/f32[64]{0:T(128)S(1)}, f32[64]{0:T(128)S(1)}) all-reduce(f32[64]{0:T(128)S(1)} %get-tuple-element.31, f32[64]{0:T(128)S(1)} %get-tuple-element.32, ...), channel_id=1, replica_groups=mesh['samp'=8,'cpg'=4] {'samp'}, use_global_device_ids=true, to_apply=%region_28.0 | all-reduce | flops 448 | bytes 3584 | tf_op jit(solution)/shard_map/psum | solution.py:99
  188.8 11.8 %all-reduce.3 = (f32[64]{0:T(128)S(1)}, f32[64]{0:T(128)S(1)}, f32[64]{0:T(128)S(1)}, f32[64]{0:T(128)S(1)}, f32[64]{0:T(128)S(1)}, /*index=5*/f32[64]{0:T(128)S(1)}, f32[64]{0:T(128)S(1)}) all-reduce(f32[64]{0:T(128)S(1)} %get-tuple-element.29, f32[64]{0:T(128)S(1)} %get-tuple-element.30, ...), channel_id=1, replica_groups=mesh['samp'=8,'cpg'=4] {'samp'}, use_global_device_ids=true, to_apply=%region_42.0 | all-reduce | flops 448 | bytes 3584 | tf_op jit(solution)/shard_map/psum | solution.py:99
  200.6 0.6 multiply_reduce_fusion.4
  201.2 11.8 %all-reduce.2 = (f32[64]{0:T(128)S(1)}, f32[64]{0:T(128)S(1)}, f32[64]{0:T(128)S(1)}, f32[64]{0:T(128)S(1)}, f32[64]{0:T(128)S(1)}, /*index=5*/f32[64]{0:T(128)S(1)}, f32[64]{0:T(128)S(1)}) all-reduce(f32[64]{0:T(128)S(1)} %get-tuple-element.27, f32[64]{0:T(128)S(1)} %get-tuple-element.28, ...), channel_id=1, replica_groups=mesh['samp'=8,'cpg'=4] {'samp'}, use_global_device_ids=true, to_apply=%region_56.0 | all-reduce | flops 448 | bytes 3584 | tf_op jit(solution)/shard_map/psum | solution.py:99
  213.9 11.8 %all-reduce.1 = (f32[64]{0:T(128)S(1)}, f32[64]{0:T(128)S(1)}) all-reduce(f32[64]{0:T(128)S(1)} %get-tuple-element.3, f32[64]{0:T(128)S(1)} %get-tuple-element.2), channel_id=1, replica_groups=mesh['samp'=8,'cpg'=4] {'samp'}, use_global_device_ids=true, to_apply=%region_58.0 | all-reduce | flops 128 | bytes 1024 | tf_op jit(solution)/shard_map/psum | solution.py:102
  225.7 3.6 %collective-permute-start = (f32[8]{0:T(128)S(1)}, f32[8]{0:T(128)S(1)}, u32[]{:S(2)}, u32[]{:S(2)}) collective-permute-start(f32[8]{0:T(128)S(1)} %get-tuple-element.81), channel_id=1, source_target_pairs={{0,1},{1,2},{2,3},{4,5},{5,6},{6,7},{8,9},{9,10},{10,11},{12,13},{... | collective-permute-start | bytes 104 | tf_op jit(solution)/shard_map/ppermute | solution.py:19
  229.4 1.3 collective-permute-start.1
  230.7 4.2 %collective-permute-done.1 = f32[8]{0:T(128)S(1)} collective-permute-done((f32[8]{0:T(128)S(1)}, f32[8]{0:T(128)S(1)}, u32[]{:S(2)}, u32[]{:S(2)}) %collective-permute-start.1) | collective-permute-done | bytes 64 | tf_op jit(solution)/shard_map/ppermute | solution.py:20
  235.0 0.6 add_divide_fusion.4
  (25 shorter events, 1.9 us)
Async XLA Ops:
  7.2 33.2 %all-gather.3.cloned.1.call-start = ((), (), s32[]{:S(2)}) async-start(), calls=%async_computation.1 | async-start | bytes 2359296 | tf_op jit(solution)/shard_map/all_gather | solution.py:90
  9.3 60.8 %all-gather.5.cloned.1.call-start = ((), (), s32[]{:S(2)}) async-start(), calls=%async_computation.2 | async-start | bytes 2359296 | tf_op jit(solution)/shard_map/all_gather | solution.py:91
  10.0 148.1 %reduce-scatter.2.cloned.1.call-start = ((), (), s32[]{:S(2)}) async-start(), calls=%async_computation.3 | async-start | bytes 5242880 | tf_op jit(solution)/shard_map/reduce_scatter | solution.py:104
  81.1 0.7 copy-start.2
  81.1 0.8 copy-start.1
  158.1 30.1 %copy-start = (f32[64,4096]{1,0:T(8,128)S(1)}, f32[64,4096]{1,0:T(8,128)}, u32[]{:S(2)}) copy-start(f32[64,4096]{1,0:T(8,128)} %reduce-scatter.2.cloned.1.call-done) | copy-start | bytes 3145732
  174.4 60.5 %copy-start.3 = (s32[64]{0:T(128)S(1)}, s32[64]{0:T(128)}, u32[]{:S(2)}) copy-start(s32[64]{0:T(128)} %param.13) | copy-start | bytes 772
  225.7 5.0 %collective-permute-start = (f32[8]{0:T(128)S(1)}, f32[8]{0:T(128)S(1)}, u32[]{:S(2)}, u32[]{:S(2)}) collective-permute-start(f32[8]{0:T(128)S(1)} %get-tuple-element.81), channel_id=1, source_target_pairs={{0,1},{1,2},{2,3},{4,5},{5,6},{6,7},{8,9},{9,10},{10,11},{12,13},{... | collective-permute-start | bytes 104 | tf_op jit(solution)/shard_map/ppermute | solution.py:19
  229.4 5.5 %collective-permute-start.1 = (f32[8]{0:T(128)S(1)}, f32[8]{0:T(128)S(1)}, u32[]{:S(2)}, u32[]{:S(2)}) collective-permute-start(f32[8]{0:T(128)S(1)} %get-tuple-element.82), channel_id=1, source_target_pairs={{1,0},{2,1},{3,2},{5,4},{6,5},{7,6},{9,8},{10,9},{11,10},{13,12},{... | collective-permute-start | bytes 104 | tf_op jit(solution)/shard_map/ppermute | solution.py:20
Sparse Core Ops, SparseCore 0:
  9.9 30.4 all-gather.2
  42.3 27.7 all-gather.4
  81.3 76.7 reduce-scatter.1
where the time goes:
time: 243 us; the launch traced here: 242 us
  waiting for transfers between devices  132 us (54%)
  blocking collectives  60.5 us (25%)
  matrix products  17.4 us (7%)
  between operations  13.8 us (6%)
  other arithmetic  11.4 us (5%)
  starting transfers between devices  5.05 us (2%)
    reduce_scatter x1, waiting for transfers between devices, shards(): lax.psum_scatter(jnp.concatenate([jnp.dot(all_resp, eigvecs, preferred_el...  75.6 us
    psum x4, blocking collectives, fit_block(): return lax.psum(partials, 'samp')  48.7 us
    all_gather x1, waiting for transfers between devices, shards(): lax.all_gather(weighted, 'samp', axis=0, tiled=True)  30.3 us
    all_gather x1, waiting for transfers between devices, shards(): lax.all_gather(design, 'samp', axis=0, tiled=True)  21 us
    psum x1, blocking collectives, score_block(): return lax.psum(partials, 'samp')  11.8 us
    dot_general x1, matrix products, shards(): jnp.dot(all_resp, eigvecs, preferred_element_type=jnp.float32)  8.71 us
    dot_general x1, matrix products, shards(): jnp.dot(all_design, eigvecs, preferred_element_type=jnp.float32)  8.71 us
  transfers between devices with their start and end apart: 5, of which 4 were waited for; matrix products, arithmetic and copies ran while one was open for 4% of the time, Pallas kernels for 0%

commit v1 on v0

--- a/solution.py
+++ b/solution.py
@@ -87,7 +87,9 @@
     weighted = (root_weight * responses.astype(jnp.float32)).astype(jnp.bfloat16)
     design = (root_weight * phenotype[None, :]).astype(jnp.bfloat16)
     all_resp, all_design = (
-        lax.all_gather(weighted, "samp", axis=0, tiled=True),
+        jnp.concatenate(
+            lax.all_to_all(jnp.stack([weighted] * lax.axis_size("samp")), "samp", 0, 0), axis=0
+        ),
         lax.all_gather(design, "samp", axis=0, tiled=True),
     )
     cpg_count = lax.axis_size("cpg")

time: 243 us -> 229 us (0.942)
  waiting for transfers between devices: 132 us -> 79.4 us
  blocking collectives: 60.5 us -> 99.4 us
    all_to_all x0 -> x1, blocking collectives: none -> 38.9 us  [shards(): lax.all_to_all(jnp.stack([weighted] * lax.axis_size('samp')), 'samp', 0, 0)]
    all_gather x1 -> x0, waiting for transfers between devices: 30.3 us -> none  [shards(): lax.all_gather(weighted, 'samp', axis=0, tiled=True)]
    all_gather x1, waiting for transfers between devices: 21 us -> 0.02 us  [shards(): lax.all_gather(design, 'samp', axis=0, tiled=True)]
  transfers between devices with their start and end apart: 5 -> 4, of which waited for: 4 -> 2; matrix products, arithmetic and copies ran while one was open for 4% -> 4% of each run, Pallas kernels for 0% -> 0%
where the time goes in v1:
time: 229 us
  blocking collectives  99.4 us (43%)
  waiting for transfers between devices  79.4 us (35%)
  matrix products  16.9 us (7%)
  between operations  14.1 us (6%)
  other arithmetic  11.3 us (5%)
  starting transfers between devices  5.04 us (2%)
  local copies, waits for them, and re-layouts  2.35 us (1%)
    reduce_scatter x1, waiting for transfers between devices, shards(): lax.psum_scatter(jnp.concatenate([jnp.dot(all_resp, eigvecs, preferred_el...  75.2 us
    psum x4, blocking collectives, fit_block(): return lax.psum(partials, 'samp')  48.7 us
    all_to_all x1, blocking collectives, shards(): lax.all_to_all(jnp.stack([weighted] * lax.axis_size('samp')), 'samp', 0, 0)  38.9 us
    psum x1, blocking collectives, score_block(): return lax.psum(partials, 'samp')  11.8 us
    dot_general x1, matrix products, shards(): jnp.dot(all_design, eigvecs, preferred_element_type=jnp.float32)  8.73 us
    dot_general x1, matrix products, shards(): jnp.dot(all_resp, eigvecs, preferred_element_type=jnp.float32)  8.21 us
    reduce_sum x4, other arithmetic, fit_scores(): energy_part = jnp.sum(design_over * rot_design, axis=sum_axis)  4.81 us
  transfers between devices with their start and end apart: 4, of which 2 were waited for; matrix products, arithmetic and copies ran while one was open for 4% of the time, Pallas kernels for 0%

profile of v1, /device:TPU:0, one launch (start us, length us, event | category | flops | bytes accessed | tf_op | source)
XLA Modules:
  0.0 228.6 jit_solution(9924387359132329339)
XLA Ops:
  7.2 2.0 multiply_convert_fusion.1
  9.5 38.9 %all_to_all.5 = bf16[8,32,4096]{2,1,0:T(8,128)(2,1)S(1)} all-to-all(bf16[8,32,4096]{2,1,0:T(8,128)(2,1)S(1)} %stack.2), channel_id=1, replica_groups=mesh['samp'=8,'cpg'=4] {'samp'}, dimensions={0} | all-to-all | bytes 4194304 | tf_op jit(solution)/shard_map/all_to_all | solution.py:91
  48.4 8.2 %fusion.38 = f32[256,2048]{1,0:T(8,128)S(1)} fusion(bf16[256,4096]{1,0:T(8,128)(2,1)S(1)} %bitcast.5, bf16[4096,2048]{1,0:T(8,128)(2,1)} %param.10), kind=kOutput, calls=%fused_computation.110 | convolution fusion | flops 4294967296 | bytes 20971520 | tf_op jit(solution)/shard_map/dot_general | solution.py:109
  56.6 8.7 %fusion.39 = f32[256,2048]{1,0:T(8,128)S(1)} fusion(bf16[256,4096]{1,0:T(8,128)(2,1)} %all-gather.2.cloned.1.call-done, bf16[4096,2048]{1,0:T(8,128)(2,1)} %param.10), kind=kOutput, calls=%fused_computation.111 | convolution fusion | flops 4294967296 | bytes 20971520 | tf_op jit(solution)/shard_map/dot_general | solution.py:110
  65.4 2.3 %pad_maximum_fusion = f32[256,4096]{1,0:T(8,128)} fusion(f32[256,2048]{1,0:T(8,128)S(1)} %fusion.39, f32[256,2048]{1,0:T(8,128)S(1)} %fusion.38), kind=kLoop, calls=%fused_computation | loop fusion | flops 1048576 | bytes 8388608 | tf_op jit(solution)/shard_map/concatenate | solution.py:107
  67.7 0.6 copy-done.2
  68.4 0.6 multiply_multiply_fusion.14
  69.0 75.2 %reduce-scatter.2.cloned.1.call-done = f32[64,4096]{1,0:T(8,128)} async-done(((f32[256,4096]{1,0:T(8,128)}), f32[64,4096]{1,0:T(8,128)}) %reduce-scatter.2.cloned.1.call-update) | async-done | bytes 1048592 | tf_op jit(solution)/shard_map/reduce_scatter | solution.py:106
  144.3 1.7 fusion.7
  146.0 0.7 reduce_sum.280
  146.6 0.6 reduce_sum.282
  147.3 13.3 %all-reduce.5 = (f32[64]{0:T(128)S(1)}, f32[64]{0:T(128)S(1)}, f32[64]{0:T(128)S(1)}, f32[64]{0:T(128)S(1)}, f32[64]{0:T(128)S(1)}, /*index=5*/f32[64]{0:T(128)S(1)}, f32[64]{0:T(128)S(1)}) all-reduce(f32[64]{0:T(128)S(1)} %reduce_sum.282, f32[64]{0:T(128)S(1)} %reduce_sum.280, ...), channel_id=1, replica_groups=mesh['samp'=8,'cpg'=4] {'samp'}, use_global_device_ids=true, to_apply=%region_14.0 | all-reduce | flops 448 | bytes 3584 | tf_op jit(solution)/shard_map/psum | solution.py:101
  160.6 1.9 multiply_reduce_fusion.12
  162.5 11.8 %all-reduce.4 = (f32[64]{0:T(128)S(1)}, f32[64]{0:T(128)S(1)}, f32[64]{0:T(128)S(1)}, f32[64]{0:T(128)S(1)}, f32[64]{0:T(128)S(1)}, /*index=5*/f32[64]{0:T(128)S(1)}, f32[64]{0:T(128)S(1)}) all-reduce(f32[64]{0:T(128)S(1)} %get-tuple-element.31, f32[64]{0:T(128)S(1)} %get-tuple-element.32, ...), channel_id=1, replica_groups=mesh['samp'=8,'cpg'=4] {'samp'}, use_global_device_ids=true, to_apply=%region_28.0 | all-reduce | flops 448 | bytes 3584 | tf_op jit(solution)/shard_map/psum | solution.py:101
  174.3 0.6 multiply_reduce_fusion.8
  175.0 11.8 %all-reduce.3 = (f32[64]{0:T(128)S(1)}, f32[64]{0:T(128)S(1)}, f32[64]{0:T(128)S(1)}, f32[64]{0:T(128)S(1)}, f32[64]{0:T(128)S(1)}, /*index=5*/f32[64]{0:T(128)S(1)}, f32[64]{0:T(128)S(1)}) all-reduce(f32[64]{0:T(128)S(1)} %get-tuple-element.29, f32[64]{0:T(128)S(1)} %get-tuple-element.30, ...), channel_id=1, replica_groups=mesh['samp'=8,'cpg'=4] {'samp'}, use_global_device_ids=true, to_apply=%region_42.0 | all-reduce | flops 448 | bytes 3584 | tf_op jit(solution)/shard_map/psum | solution.py:101
  186.8 0.6 multiply_reduce_fusion.4
  187.4 11.8 %all-reduce.2 = (f32[64]{0:T(128)S(1)}, f32[64]{0:T(128)S(1)}, f32[64]{0:T(128)S(1)}, f32[64]{0:T(128)S(1)}, f32[64]{0:T(128)S(1)}, /*index=5*/f32[64]{0:T(128)S(1)}, f32[64]{0:T(128)S(1)}) all-reduce(f32[64]{0:T(128)S(1)} %get-tuple-element.27, f32[64]{0:T(128)S(1)} %get-tuple-element.28, ...), channel_id=1, replica_groups=mesh['samp'=8,'cpg'=4] {'samp'}, use_global_device_ids=true, to_apply=%region_56.0 | all-reduce | flops 448 | bytes 3584 | tf_op jit(solution)/shard_map/psum | solution.py:101
  199.2 0.5 fusion.32
  200.0 11.8 %all-reduce.1 = (f32[64]{0:T(128)S(1)}, f32[64]{0:T(128)S(1)}) all-reduce(f32[64]{0:T(128)S(1)} %get-tuple-element.3, f32[64]{0:T(128)S(1)} %get-tuple-element.2), channel_id=1, replica_groups=mesh['samp'=8,'cpg'=4] {'samp'}, use_global_device_ids=true, to_apply=%region_58.0 | all-reduce | flops 128 | bytes 1024 | tf_op jit(solution)/shard_map/psum | solution.py:104
  211.9 3.7 %collective-permute-start = (f32[8]{0:T(128)S(1)}, f32[8]{0:T(128)S(1)}, u32[]{:S(2)}, u32[]{:S(2)}) collective-permute-start(f32[8]{0:T(128)S(1)} %get-tuple-element.81), channel_id=1, source_target_pairs={{0,1},{1,2},{2,3},{4,5},{5,6},{6,7},{8,9},{9,10},{10,11},{12,13},{... | collective-permute-start | bytes 104 | tf_op jit(solution)/shard_map/ppermute | solution.py:19
  215.6 1.3 collective-permute-start.1
  216.9 4.2 %collective-permute-done.1 = f32[8]{0:T(128)S(1)} collective-permute-done((f32[8]{0:T(128)S(1)}, f32[8]{0:T(128)S(1)}, u32[]{:S(2)}, u32[]{:S(2)}) %collective-permute-start.1) | collective-permute-done | bytes 64 | tf_op jit(solution)/shard_map/ppermute | solution.py:20
  221.1 0.6 add_divide_fusion.4
  (24 shorter events, 1.0 us)
Async XLA Ops:
  7.2 49.5 %all-gather.2.cloned.1.call-start = ((), (), s32[]{:S(2)}) async-start(), calls=%async_computation.2 | async-start | bytes 2359296 | tf_op jit(solution)/shard_map/all_gather | solution.py:93
  9.2 135.1 %reduce-scatter.2.cloned.1.call-start = ((), (), s32[]{:S(2)}) async-start(), calls=%async_computation.3 | async-start | bytes 5242880 | tf_op jit(solution)/shard_map/reduce_scatter | solution.py:106
  67.6 0.7 copy-start.2
  67.7 0.8 copy-start.1
  144.3 30.1 %copy-start = (f32[64,4096]{1,0:T(8,128)S(1)}, f32[64,4096]{1,0:T(8,128)}, u32[]{:S(2)}) copy-start(f32[64,4096]{1,0:T(8,128)} %reduce-scatter.2.cloned.1.call-done) | copy-start | bytes 3145732
  160.6 60.5 %copy-start.3 = (s32[64]{0:T(128)S(1)}, s32[64]{0:T(128)}, u32[]{:S(2)}) copy-start(s32[64]{0:T(128)} %param.13) | copy-start | bytes 772
  211.9 5.0 %collective-permute-start = (f32[8]{0:T(128)S(1)}, f32[8]{0:T(128)S(1)}, u32[]{:S(2)}, u32[]{:S(2)}) collective-permute-start(f32[8]{0:T(128)S(1)} %get-tuple-element.81), channel_id=1, source_target_pairs={{0,1},{1,2},{2,3},{4,5},{5,6},{6,7},{8,9},{9,10},{10,11},{12,13},{... | collective-permute-start | bytes 104 | tf_op jit(solution)/shard_map/ppermute | solution.py:19
  215.6 5.5 %collective-permute-start.1 = (f32[8]{0:T(128)S(1)}, f32[8]{0:T(128)S(1)}, u32[]{:S(2)}, u32[]{:S(2)}) collective-permute-start(f32[8]{0:T(128)S(1)} %get-tuple-element.82), channel_id=1, source_target_pairs={{1,0},{2,1},{3,2},{5,4},{6,5},{7,6},{9,8},{10,9},{11,10},{13,12},{... | collective-permute-start | bytes 104 | tf_op jit(solution)/shard_map/ppermute | solution.py:20
Sparse Core Ops, SparseCore 0:
  9.9 40.2 all-gather.1
  67.8 76.4 reduce-scatter.1
